TPU v7x, 128 devices: a whole 4x4x4 slice. The times are simulated.
128 devices in a mesh: rhs: 1, col: 64 (over z, y, x), row: 2 (over core).
Axes of the slice: x: 4, y: 4, z: 4, core: 2. Of those that a mesh axis runs over, the one named last changes fastest.
Arguments:
- volume: bfloat16 [128, 128, 128, 64], P('row', 'col', None, 'rhs')
- a_one: bfloat16 [128, 128], replicated
- b_one: bfloat16 [128, 128], replicated
- a_two: bfloat16 [128, 128], replicated
- b_two: bfloat16 [128, 128], replicated
- a_three: bfloat16 [128, 128], replicated
- b_three: bfloat16 [128, 128], replicated
- spectrum: float32 [128, 128, 128], P('row', 'col')
Outputs:
- output: float32 [128, 128, 128, 64], P('row', 'col', None, 'rhs')
All inputs are finite; a program needn't handle non-finite values.
Results may differ from a plain program's by a relative error of at most 0.0126449.
Values are sent between devices in bfloat16 or wider.
A program may use at most 1 GiB of HBM per device.

v0:
```python
import jax
import jax.numpy as jnp
from jax import lax
from jax.sharding import PartitionSpec as P


def mode_product(factor, tensor, form):
    return jnp.einsum(form, factor, tensor, preferred_element_type=jnp.float32)


def solution(mesh):
    vol_spec = P('row', 'col', None, 'rhs')
    diag_spec = P('row', 'col', None)
    full_spec = P(None, None)

    def local_op(volume, a_one, b_one, a_two, b_two, a_three, b_three, spectrum):
        u_three = mode_product(a_three, volume, 'ka,ijar->ijkr').astype(jnp.bfloat16)
        one_whole = lax.all_to_all(u_three, 'row', 2, 0, tiled=True)
        u_one = mode_product(a_one, one_whole, 'ia,ajkr->ijkr').astype(jnp.bfloat16)
        two_whole = lax.all_to_all(u_one, 'col', 0, 1, tiled=True)
        u_two = mode_product(a_two, two_whole, 'ja,iakr->ijkr').astype(jnp.bfloat16)
        diag_mid = lax.all_to_all(spectrum, 'row', 2, 0, tiled=True)
        diag_new = lax.all_to_all(diag_mid, 'col', 0, 1, tiled=True)
        scaled = (diag_new[:, :, :, None] * u_two.astype(jnp.float32)).astype(jnp.bfloat16)
        v_two = mode_product(b_two, scaled, 'ja,iakr->ijkr').astype(jnp.bfloat16)
        one_again = lax.all_to_all(v_two, 'col', 1, 0, tiled=True)
        v_one = mode_product(b_one, one_again, 'ia,ajkr->ijkr').astype(jnp.bfloat16)
        three_whole = lax.all_to_all(v_one, 'row', 0, 2, tiled=True)
        return mode_product(b_three, three_whole, 'ka,ijar->ijkr')

    return jax.shard_map(local_op, mesh=mesh, in_specs=(vol_spec, full_spec, full_spec, full_spec, full_spec, full_spec, full_spec, diag_spec), out_specs=vol_spec, check_vma=False)
```

profile of v0, /device:TPU:1, one launch (start us, length us, event | category | flops | bytes accessed | tf_op | source)
XLA Modules:
  0.0 261.6 jit_solution(6583639797833607294)
XLA Ops:
  0.0 1.1 copy.40
  1.9 4.6 %all-to-all-start = ((f32[2,1,8192]{2,1,0:T(1,128)}), f32[2,1,8192]{2,1,0:T(1,128)S(1)}, u32[]{:S(2)}, u32[]{:S(2)}) async-start(f32[2,1,8192]{2,1,0:T(1,128)} %reshape.12), calls=%async_computation | async-start | bytes 131072 | tf_op jit(solution)/shard_map/all_to_all | solution.py:22
  6.5 2.8 %convert_bitcast_fusion.3 = bf16[64,2,128,64]{2,3,1,0:T(8,128)(2,1)} fusion(bf16[64,2,128,64]{2,3,1,0:T(8,128)(2,1)S(1)} %copy-done, bf16[128,128]{1,0:T(8,128)(2,1)} %param.13), kind=kOutput, calls=%fused_computation.12 | convolution fusion | flops 269484032 | bytes 4227072 | tf_op jit(solution)/shard_map/ka,ijar->ijkr/dot_general | solution.py:8
  9.3 9.4 %copy.46 = bf16[64,2,128,64]{3,1,0,2:T(2,128)(2,1)} copy(bf16[64,2,128,64]{2,3,1,0:T(8,128)(2,1)} %convert_bitcast_fusion.3) | data formatting | bytes 4194304 | tf_op jit(solution)/shard_map/convert_element_type | solution.py:17
  18.7 5.9 %reshape.8 = bf16[2,2,262144]{2,1,0:T(2,128)(2,1)} reshape(bf16[128,64,2,64]{3,2,1,0:T(2,128)(2,1)} %bitcast.82) | data formatting | bytes 4194304
  24.6 3.8 %all-to-all-start.2 = ((bf16[2,2,262144]{2,1,0:T(2,128)(2,1)}), bf16[2,2,262144]{2,1,0:T(2,128)(2,1)S(1)}, u32[]{:S(2)}, u32[]{:S(2)}) async-start(bf16[2,2,262144]{2,1,0:T(2,128)(2,1)} %reshape.8), calls=%async_computation.2 | async-start | bytes 4194304 | tf_op jit(solution)/shard_map/all_to_all | solution.py:18
  28.9 0.9 reduce
  30.9 11.3 %all-to-all-start.1 = ((f32[64,1,256]{2,1,0:T(1,128)}), f32[64,1,256]{2,1,0:T(1,128)S(1)}, u32[]{:S(2)}, u32[]{:S(2)}) async-start(f32[64,1,256]{2,1,0:T(1,128)} %reshape.14), calls=%async_computation.1 | async-start | bytes 131072 | tf_op jit(solution)/shard_map/all_to_all | solution.py:23
  42.2 3.9 %reshape.9 = bf16[128,64,2,64]{3,2,1,0:T(2,128)(2,1)} reshape(bf16[2,2,262144]{2,1,0:T(2,128)(2,1)S(1)} %all-to-all-done.2) | data formatting | bytes 4194304
  46.1 14.9 %copy.47 = bf16[64,2,2,64,64]{0,2,4,3,1:T(2,128)(2,1)} copy(bf16[64,2,2,64,64]{4,1,0,3,2:T(2,128)(2,1)} %bitcast.84) | data formatting | bytes 4194304 | tf_op jit(solution)/shard_map/all_to_all | solution.py:18
  60.9 6.8 %all_to_all.86 = bf16[128,2,64,64]{0,3,2,1:T(8,128)(2,1)S(1)} reshape(bf16[2,64,2,64,64]{1,0,4,3,2:T(2,128)(2,1)} %bitcast.85) | data formatting | bytes 4194304 | tf_op jit(solution)/shard_map/all_to_all | solution.py:18
  67.8 2.1 convert_bitcast_fusion.2
  69.8 7.4 %copy.48 = bf16[128,2,64,64]{3,2,1,0:T(8,128)(2,1)} copy(bf16[128,2,64,64]{0,3,2,1:T(8,128)(2,1)} %convert_bitcast_fusion.2) | data formatting | bytes 4194304 | tf_op jit(solution)/shard_map/convert_element_type | solution.py:19
  77.2 7.9 %reshape.10 = bf16[64,2,8192]{2,1,0:T(2,128)(2,1)} reshape(bf16[128,2,64,64]{3,2,1,0:T(8,128)(2,1)} %copy.48) | data formatting | bytes 4194304
  85.1 10.0 %all-to-all-start.3 = ((bf16[64,2,8192]{2,1,0:T(2,128)(2,1)}), bf16[64,2,8192]{2,1,0:T(2,128)(2,1)S(1)}, u32[]{:S(2)}, u32[]{:S(2)}) async-start(bf16[64,2,8192]{2,1,0:T(2,128)(2,1)} %reshape.10), calls=%async_computation.3 | async-start | bytes 4194304 | tf_op jit(solution)/shard_map/all_to_all | solution.py:20
  96.2 31.5 %all-to-all-done.3 = bf16[64,2,8192]{2,1,0:T(2,128)(2,1)S(1)} async-done(((bf16[64,2,8192]{2,1,0:T(2,128)(2,1)}), bf16[64,2,8192]{2,1,0:T(2,128)(2,1)S(1)}, u32[]{:S(2)}, u32[]{:S(2)}) %all-to-all-start.3) | async-done | bytes 2097184 | tf_op jit(solution)/shard_map/all_to_all | solution.py:20
  127.7 4.0 %reshape.11 = bf16[128,2,64,64]{3,2,1,0:T(8,128)(2,1)} reshape(bf16[64,2,8192]{2,1,0:T(2,128)(2,1)S(1)} %all-to-all-done.3) | data formatting | bytes 4194304
  131.7 6.0 %copy.49 = bf16[2,64,2,64,64]{4,3,2,1,0:T(8,128)(2,1)} copy(bf16[2,64,2,64,64]{4,3,2,0,1:T(8,128)(2,1)} %bitcast.86) | data formatting | bytes 4194304 | tf_op jit(solution)/shard_map/all_to_all | solution.py:20
  137.7 6.3 %convert_bitcast_fusion.1 = bf16[2,128,64,64]{1,3,2,0:T(8,128)(2,1)S(1)} fusion(bf16[2,128,64,64]{3,2,1,0:T(8,128)(2,1)} %bitcast.91, f32[2,128,64]{1,2,0:T(8,128)S(1)} %copy.45, bf16[128,128]{1,0:T(8,128)(2,1)S(1)} %copy-done.5, bf16[128,128]{1,0:T(8,128)(2,1)S(1)} %copy-done.6), kind=kOutput, calls=%fused_computation.9 | convolution fusion | flops 542113792 | bytes 4325376 | tf_op jit(solution)/shard_map/ja,iakr->ijkr/dot_general | solution.py:8
  144.0 6.4 %copy.51 = bf16[2,128,64,64]{3,2,0,1:T(8,128)(2,1)} copy(bf16[2,128,64,64]{1,3,2,0:T(8,128)(2,1)S(1)} %convert_bitcast_fusion.1) | data formatting | bytes 4194304 | tf_op jit(solution)/shard_map/convert_element_type | solution.py:25
  150.4 6.8 %reshape.16 = bf16[64,2,8192]{2,1,0:T(2,128)(2,1)S(1)} reshape(bf16[128,2,64,64]{3,2,1,0:T(8,128)(2,1)} %bitcast.83) | data formatting | bytes 4194304
  157.2 39.3 %all_to_all.105 = bf16[64,2,8192]{2,1,0:T(2,128)(2,1)} all-to-all(bf16[64,2,8192]{2,1,0:T(2,128)(2,1)S(1)} %reshape.16), channel_id=1, replica_groups=mesh['rhs'=1,'col'=64,'row'=2] {'col'}, dimensions={0} | all-to-all | bytes 4194304 | tf_op jit(solution)/shard_map/all_to_all | solution.py:26
  196.6 7.9 %reshape.17 = bf16[128,2,64,64]{3,2,1,0:T(8,128)(2,1)} reshape(bf16[64,2,8192]{2,1,0:T(2,128)(2,1)} %all_to_all.105) | data formatting | bytes 4194304
  204.5 3.2 %copy.53 = bf16[64,2,2,64,64]{4,3,2,1,0:T(8,128)(2,1)S(1)} copy(bf16[64,2,2,64,64]{4,3,1,2,0:T(8,128)(2,1)} %bitcast.87) | data formatting | bytes 4194304 | tf_op jit(solution)/shard_map/all_to_all | solution.py:26
  207.7 5.2 %convert_bitcast_fusion = bf16[128,2,64,64]{0,3,2,1:T(8,128)(2,1)S(1)} fusion(bf16[128,2,64,64]{3,2,1,0:T(8,128)(2,1)S(1)} %bitcast.88, bf16[128,128]{1,0:T(8,128)(2,1)S(1)} %copy-done.3), kind=kOutput, calls=%fused_computation.8 | convolution fusion | flops 269484032 | bytes 4227072 | tf_op jit(solution)/shard_map/ia,ajkr->ijkr/dot_general | solution.py:8
  212.8 6.4 %copy.55 = bf16[128,2,64,64]{3,2,1,0:T(8,128)(2,1)} copy(bf16[128,2,64,64]{0,3,2,1:T(8,128)(2,1)S(1)} %convert_bitcast_fusion) | data formatting | bytes 4194304 | tf_op jit(solution)/shard_map/convert_element_type | solution.py:27
  219.2 4.9 %reshape.18 = bf16[2,2,262144]{2,1,0:T(2,128)(2,1)S(1)} reshape(bf16[128,2,64,64]{3,2,1,0:T(8,128)(2,1)} %copy.55) | data formatting | bytes 4194304
  224.1 8.5 %all_to_all.106 = bf16[2,2,262144]{2,1,0:T(2,128)(2,1)} all-to-all(bf16[2,2,262144]{2,1,0:T(2,128)(2,1)S(1)} %reshape.18), channel_id=1, replica_groups=mesh['rhs'=1,'col'=64,'row'=2] {'row'}, dimensions={0} | all-to-all | bytes 4194304 | tf_op jit(solution)/shard_map/all_to_all | solution.py:28
  232.6 5.7 %reshape.19 = bf16[128,2,64,64]{3,2,1,0:T(8,128)(2,1)} reshape(bf16[2,2,262144]{2,1,0:T(2,128)(2,1)} %all_to_all.106) | data formatting | bytes 4194304
  238.2 11.1 %copy.56 = bf16[2,64,2,64,64]{3,0,4,2,1:T(2,128)(2,1)} copy(bf16[2,64,2,64,64]{4,3,2,1,0:T(8,128)(2,1)} %bitcast.89) | data formatting | bytes 4194304 | tf_op jit(solution)/shard_map/all_to_all | solution.py:28
  249.3 7.9 %all_to_all.98 = bf16[64,2,128,64]{2,3,1,0:T(8,128)(2,1)} reshape(bf16[64,2,2,64,64]{3,2,4,1,0:T(2,128)(2,1)} %bitcast.90) | data formatting | bytes 4194304 | tf_op jit(solution)/shard_map/all_to_all | solution.py:28
  257.3 4.3 %convolution_bitcast_fusion = f32[64,2,128,64]{2,3,1,0:T(8,128)} fusion(bf16[64,2,128,64]{2,3,1,0:T(8,128)(2,1)} %all_to_all.98, bf16[128,128]{1,0:T(8,128)(2,1)S(1)} %copy-done.4), kind=kOutput, calls=%fused_computation.6 | convolution fusion | flops 268435456 | bytes 6324224 | tf_op jit(solution)/shard_map/ka,ijar->ijkr/dot_general | solution.py:8
  (27 shorter events, 3.6 us)
Async XLA Ops:
  0.0 6.5 %copy-start = (bf16[64,2,128,64]{2,3,1,0:T(8,128)(2,1)S(1)}, bf16[64,2,128,64]{2,3,1,0:T(8,128)(2,1)}, u32[]{:S(2)}) copy-start(bf16[64,2,128,64]{2,3,1,0:T(8,128)(2,1)} %param.8) | copy-start | bytes 6291460
  1.9 22.7 %all-to-all-start = ((f32[2,1,8192]{2,1,0:T(1,128)}), f32[2,1,8192]{2,1,0:T(1,128)S(1)}, u32[]{:S(2)}, u32[]{:S(2)}) async-start(f32[2,1,8192]{2,1,0:T(1,128)} %reshape.12), calls=%async_computation | async-start | bytes 131072 | tf_op jit(solution)/shard_map/all_to_all | solution.py:22
  24.6 6.3 %all-to-all-start.2 = ((bf16[2,2,262144]{2,1,0:T(2,128)(2,1)}), bf16[2,2,262144]{2,1,0:T(2,128)(2,1)S(1)}, u32[]{:S(2)}, u32[]{:S(2)}) async-start(bf16[2,2,262144]{2,1,0:T(2,128)(2,1)} %reshape.8), calls=%async_computation.2 | async-start | bytes 4194304 | tf_op jit(solution)/shard_map/all_to_all | solution.py:18
  30.9 54.2 %all-to-all-start.1 = ((f32[64,1,256]{2,1,0:T(1,128)}), f32[64,1,256]{2,1,0:T(1,128)S(1)}, u32[]{:S(2)}, u32[]{:S(2)}) async-start(f32[64,1,256]{2,1,0:T(1,128)} %reshape.14), calls=%async_computation.1 | async-start | bytes 131072 | tf_op jit(solution)/shard_map/all_to_all | solution.py:23
  60.9 6.8 %copy-start.2 = (bf16[128,128]{1,0:T(8,128)(2,1)S(1)}, bf16[128,128]{1,0:T(8,128)(2,1)}, u32[]{:S(2)}) copy-start(bf16[128,128]{1,0:T(8,128)(2,1)} %param.9) | copy-start | bytes 98308
  85.1 42.6 %all-to-all-start.3 = ((bf16[64,2,8192]{2,1,0:T(2,128)(2,1)}), bf16[64,2,8192]{2,1,0:T(2,128)(2,1)S(1)}, u32[]{:S(2)}, u32[]{:S(2)}) async-start(bf16[64,2,8192]{2,1,0:T(2,128)(2,1)} %reshape.10), calls=%async_computation.3 | async-start | bytes 4194304 | tf_op jit(solution)/shard_map/all_to_all | solution.py:20
  131.7 6.0 %copy-start.5 = (bf16[128,128]{1,0:T(8,128)(2,1)S(1)}, bf16[128,128]{1,0:T(8,128)(2,1)}, u32[]{:S(2)}) copy-start(bf16[128,128]{1,0:T(8,128)(2,1)} %param.12) | copy-start | bytes 98308
  131.7 6.0 %copy-start.6 = (bf16[128,128]{1,0:T(8,128)(2,1)S(1)}, bf16[128,128]{1,0:T(8,128)(2,1)}, u32[]{:S(2)}) copy-start(bf16[128,128]{1,0:T(8,128)(2,1)} %param.11) | copy-start | bytes 98308
  204.5 3.2 %copy-start.3 = (bf16[128,128]{1,0:T(8,128)(2,1)S(1)}, bf16[128,128]{1,0:T(8,128)(2,1)}, u32[]{:S(2)}) copy-start(bf16[128,128]{1,0:T(8,128)(2,1)} %param.10) | copy-start | bytes 98308
  249.3 7.9 %copy-start.4 = (bf16[128,128]{1,0:T(8,128)(2,1)S(1)}, bf16[128,128]{1,0:T(8,128)(2,1)}, u32[]{:S(2)}) copy-start(bf16[128,128]{1,0:T(8,128)(2,1)} %param.14) | copy-start | bytes 98308
  249.3 12.2 %copy-start.1 = (bf16[64,2,128,64]{2,3,1,0:T(8,128)(2,1)S(1)}, bf16[64,2,128,64]{2,3,1,0:T(8,128)(2,1)}, u32[]{:S(2)}) copy-start(bf16[64,2,128,64]{2,3,1,0:T(8,128)(2,1)} %param.8) | copy-start | bytes 6291460
where the time goes:
time: 265 us; the launch traced here: 262 us
  local copies, waits for them, and re-layouts  130 us (49%)
  blocking collectives  47.8 us (18%)
  waiting for transfers between devices  31.5 us (12%)
  starting transfers between devices  29.7 us (11%)
  matrix products  20.6 us (8%)
    unnamed x27, local copies, waits for them, and re-layouts  49.9 us
    all_to_all x1, blocking collectives, local_op(): one_again = lax.all_to_all(v_two, 'col', 1, 0, tiled=True)  39.3 us
    all_to_all x1, waiting for transfers between devices, local_op(): two_whole = lax.all_to_all(u_one, 'col', 0, 1, tiled=True)  31.5 us
    all_to_all x2, local copies, waits for them, and re-layouts, local_op(): one_whole = lax.all_to_all(u_three, 'row', 2, 0, tiled=True)  21.7 us
    dot_general x5, matrix products, mode_product(): return jnp.einsum(form, factor, tensor, preferred_element_type=jnp.float32)  20.6 us
    all_to_all x2, local copies, waits for them, and re-layouts, local_op(): three_whole = lax.all_to_all(v_one, 'row', 0, 2, tiled=True)  19 us
    all_to_all x1, starting transfers between devices, local_op(): diag_new = lax.all_to_all(diag_mid, 'col', 0, 1, tiled=True)  11.3 us
    all_to_all x1, starting transfers between devices, local_op(): two_whole = lax.all_to_all(u_one, 'col', 0, 1, tiled=True)  9.96 us
  transfers between devices with their start and end apart: 4, of which 1 were waited for; matrix products, arithmetic and copies ran while one was open for 22% of the time, Pallas kernels for 0%

commit v1 on v0

v1 whole, which is shorter than its diff:
```python
import functools

import jax
import jax.numpy as jnp
from jax import lax
from jax.experimental import pallas as pl
from jax.experimental.pallas import tpu as pltpu
from jax.sharding import PartitionSpec as P

MESH = pl.DeviceIdType.MESH
BF = jnp.bfloat16
F32 = jnp.float32
N = 128
C = 64
NCH = 4
R = C // NCH
HALF = N // 2
STEP = 37


def partner_at(t, col, row):
    off = lax.rem(t * STEP, N)
    row2 = lax.rem(row + off, 2)
    x = lax.rem(lax.rem(col, 4) + off // 2, 4)
    y = lax.rem(lax.rem(col // 4, 4) + off // 8, 4)
    z = lax.rem(col // 16 + off // 32, 4)
    return z * 16 + y * 4 + x, row2


def by_rows(factor, stack):
    for r in range(0, stack.shape[0], 2):
        pair = jnp.concatenate([stack[r], stack[r + 1]], axis=1)
        yield jnp.dot(factor, pair, preferred_element_type=F32)


def restack(products):
    parts = []
    for p in products:
        parts += [p[:, :N], p[:, N:]]
    return jnp.swapaxes(jnp.stack(parts, axis=0), 0, 1)


def exchange_kernel(x_ref, a1_ref, b1_ref, a2_ref, b2_ref, a3_ref, d_ref, v_ref,
                    xv, us, uu, m1, r1, m2, r2, vs, dv,
                    xsem, us_s, us_r, d_s, d_r, s1, q1, s2, q2, v_s, v_r, o_s):
    col, row = lax.axis_index("col"), lax.axis_index("row")
    me = col * 2 + row

    loads = []
    for k in range(2):
        j = (1 - row) if k == 0 else row
        load = pltpu.make_async_copy(x_ref.at[:, pl.ds(j, 1)], xv.at[:, pl.ds(k, 1)], xsem.at[k])
        load.start()
        loads.append(load)

    barrier = pltpu.get_barrier_semaphore()

    def greet(t, carry):
        c2, g2 = partner_at(t, col, row)
        pl.semaphore_signal(barrier, inc=1, device_id=(0, c2, g2), device_id_type=MESH)
        return carry

    lax.fori_loop(1, N, greet, 0)

    def mode_three(k, block, out):
        rows = xv[pl.ds(block * 16, 16), k].reshape(16 * C, N)
        u = lax.dot_general(rows, a3_ref[...], (((1,), (1,)), ((), ())), preferred_element_type=F32)
        out[pl.ds(block * 16 + (0 if k == 0 else row * HALF), 16)] = u.astype(BF).reshape(16, C, N)

    loads[0].wait()

    def three_a(b, carry):
        mode_three(0, b, us)
        return carry

    lax.fori_loop(0, 4, three_a, 0)
    loads[1].wait()

    def three_b(b, carry):
        mode_three(1, b, uu)
        return carry

    lax.fori_loop(0, 4, three_b, 0)

    pl.semaphore_wait(barrier, N - 1)

    def swap_u(ch):
        part = pl.ds(pl.multiple_of(ch * R, R), R)
        return pltpu.make_async_remote_copy(
            src_ref=us.at[:, part], dst_ref=uu.at[pl.ds(row * HALF, HALF), part],
            send_sem=us_s.at[ch], recv_sem=us_r.at[ch],
            device_id=(0, col, 1 - row), device_id_type=MESH)

    for ch in range(NCH):
        swap_u(ch).start()

    def send_d(t, carry):
        i = lax.rem(t * STEP, HALF)
        target = row * HALF + i

        @pl.when(target != me)
        def _():
            pltpu.make_async_remote_copy(
                src_ref=d_ref.at[i], dst_ref=dv.at[col], send_sem=d_s, recv_sem=d_r,
                device_id=(0, target // 2, lax.rem(target, 2)), device_id_type=MESH).start()

        @pl.when(target == me)
        def _():
            dv[col] = d_ref[i]

        return carry

    lax.fori_loop(0, HALF, send_d, 0)

    def fan_out(ch, src, dst, ssem, rsem):
        def body(t, carry):
            c2, g2 = partner_at(t, col, row)
            pltpu.make_async_remote_copy(
                src_ref=src.at[ch, c2 * 2 + g2], dst_ref=dst.at[ch, me],
                send_sem=ssem.at[ch], recv_sem=rsem.at[ch],
                device_id=(0, c2, g2), device_id_type=MESH).start()
            return carry

        lax.fori_loop(1, N, body, 0)
        dst[ch, me] = src[ch, me]

    def wait_all(buf, ch, sem):
        whole = buf.at[ch, pl.ds(0, N - 1)]
        pltpu.make_async_copy(whole, whole, sem.at[ch]).wait()

    def first(ch, carry):
        swap_u(ch).wait_recv()
        part = pl.ds(pl.multiple_of(ch * R, R), R)
        stack = jnp.swapaxes(uu[:, part], 0, 1)
        m1[ch] = restack(p.astype(BF) for p in by_rows(a1_ref[...], stack))
        fan_out(ch, m1, r1, s1, q1)
        return carry

    lax.fori_loop(0, NCH, first, 0)

    mine = row == col // (HALF // 2)

    @pl.when(mine)
    def _():
        part = dv.at[pl.ds(0, HALF - 1)]
        pltpu.make_async_copy(part, part, d_r).wait()

    @pl.when(jnp.logical_not(mine))
    def _():
        pltpu.make_async_copy(dv, dv, d_r).wait()

    def second(ch, carry):
        wait_all(r1, ch, q1)
        diag = dv[...].reshape(N, N)
        diag = jnp.concatenate([diag, diag], axis=1)
        stack = jnp.swapaxes(r1[ch], 0, 1)
        outs = []
        for p in by_rows(a2_ref[...], stack):
            w = (diag * p.astype(BF).astype(F32)).astype(BF)
            outs.append(jnp.dot(b2_ref[...], w, preferred_element_type=F32).astype(BF))
        m2[ch] = restack(outs)
        fan_out(ch, m2, r2, s2, q2)
        return carry

    lax.fori_loop(0, NCH, second, 0)

    def swap_v(ch):
        part = pl.ds(pl.multiple_of(ch * R, R), R)
        return pltpu.make_async_remote_copy(
            src_ref=vs.at[pl.ds((1 - row) * HALF, HALF), part], dst_ref=v_ref.at[row, :, part],
            send_sem=v_s.at[ch], recv_sem=v_r.at[ch],
            device_id=(0, col, 1 - row), device_id_type=MESH)

    def keep_v(ch):
        part = pl.ds(pl.multiple_of(ch * R, R), R)
        return pltpu.make_async_copy(
            vs.at[pl.ds(row * HALF, HALF), part], v_ref.at[row, :, part], o_s.at[ch])

    def third(ch, carry):
        wait_all(r2, ch, q2)
        part = pl.ds(pl.multiple_of(ch * R, R), R)
        stack = jnp.swapaxes(r2[ch], 0, 1)
        vs[:, part] = restack(p.astype(BF) for p in by_rows(b1_ref[...], stack))
        swap_v(ch).start()
        keep_v(ch).start()
        return carry

    lax.fori_loop(0, NCH, third, 0)

    @pl.when(mine)
    def _():
        part = dv.at[pl.ds(0, HALF - 1)]
        pltpu.make_async_copy(part, part, d_s).wait()

    @pl.when(jnp.logical_not(mine))
    def _():
        pltpu.make_async_copy(dv, dv, d_s).wait()

    def drain(ch, carry):
        swap_u(ch).wait_send()
        wait_all(m1, ch, s1)
        wait_all(m2, ch, s2)
        swap_v(ch).wait()
        keep_v(ch).wait()
        return carry

    lax.fori_loop(0, NCH, drain, 0)


def exchange(x, a1, b1, a2, b2, a3, d):
    dma = pltpu.SemaphoreType.DMA
    vmem = pl.BlockSpec(memory_space=pltpu.VMEM)
    hbm = pl.BlockSpec(memory_space=pl.ANY)
    return pl.pallas_call(
        exchange_kernel,
        out_shape=jax.ShapeDtypeStruct((2, HALF, C, N), BF),
        in_specs=[hbm] + [vmem] * 6,
        out_specs=hbm,
        scratch_shapes=[
            pltpu.VMEM((HALF, 2, C, N), BF),
            pltpu.VMEM((HALF, C, N), BF),
            pltpu.VMEM((N, C, N), BF),
            pltpu.VMEM((NCH, N, R, N), BF),
            pltpu.VMEM((NCH, N, R, N), BF),
            pltpu.VMEM((NCH, N, R, N), BF),
            pltpu.VMEM((NCH, N, R, N), BF),
            pltpu.VMEM((N, C, N), BF),
            pltpu.VMEM((HALF, 2, N), F32),
            dma((2,)), dma((NCH,)), dma((NCH,)), dma, dma,
            dma((NCH,)), dma((NCH,)), dma((NCH,)), dma((NCH,)),
            dma((NCH,)), dma((NCH,)), dma((NCH,)),
        ],
        compiler_params=pltpu.CompilerParams(
            collective_id=0, has_side_effects=True, vmem_limit_bytes=40 << 20),
        name="exchange",
    )(x, a1, b1, a2, b2, a3, d)


def last_kernel(v_ref, b3_ref, z_ref):
    for j in range(2):
        rows = v_ref[j].reshape(-1, N)
        z = lax.dot_general(rows, b3_ref[...], (((1,), (1,)), ((), ())), preferred_element_type=F32)
        z_ref[:, j] = z.reshape(z_ref.shape[0], C, N)


def last(v, b3):
    step = 8
    return pl.pallas_call(
        last_kernel,
        grid=(HALF // step,),
        out_shape=jax.ShapeDtypeStruct((HALF, 2, C, N), F32),
        in_specs=[pl.BlockSpec((2, step, C, N), lambda i: (0, i, 0, 0)),
                  pl.BlockSpec((N, N), lambda i: (0, 0))],
        out_specs=pl.BlockSpec((step, 2, C, N), lambda i: (i, 0, 0, 0)),
        name="last",
    )(v, b3)


def solution(mesh):
    vol_spec = P("row", "col", None, "rhs")
    diag_spec = P("row", "col", None)
    full = P(None, None)

    def local_op(volume, a_one, b_one, a_two, b_two, a_three, b_three, spectrum):
        x = jnp.swapaxes(volume, 2, 3)
        v = exchange(x, a_one, b_one, a_two, b_two, a_three, spectrum)
        return jnp.swapaxes(last(v, b_three), 2, 3)

    return jax.shard_map(local_op, mesh=mesh, in_specs=(vol_spec,) + (full,) * 6 + (diag_spec,),
                         out_specs=vol_spec, check_vma=False)
```

time: 265 us -> 82.7 us (0.31); the launches traced: 262 us -> 82.1 us
  local copies, waits for them, and re-layouts: 130 us -> 7.56 us
  Pallas kernels: 0 us -> 74.5 us
  blocking collectives: 47.8 us -> 0 us
  waiting for transfers between devices: 31.5 us -> 0 us
  starting transfers between devices: 29.7 us -> 0 us
  matrix products: 20.6 us -> 0 us
    pallas_call x0 -> x2, Pallas kernels: none -> 74.5 us  [the longest x1 67.7 us: exchange(): pl.pallas_call(exchange_kernel, out_shape=jax.ShapeDtypeStruct((2, HALF,...]
    all_to_all x10 -> x0, local copies, waits for them, and re-layouts: 50.7 us -> none  [the longest x2 21.7 us: local_op(): one_whole = lax.all_to_all(u_three, 'row', 2, 0, tiled=True)]
    all_to_all x2 -> x0, blocking collectives: 47.8 us -> none  [the longest x1 39.3 us: local_op(): one_again = lax.all_to_all(v_two, 'col', 1, 0, tiled=True)]
    unnamed x27 -> x16, local copies, waits for them, and re-layouts: 49.9 us -> 7.56 us
    all_to_all x4 -> x0, waiting for transfers between devices: 31.5 us -> none  [the longest x1 31.5 us: local_op(): two_whole = lax.all_to_all(u_one, 'col', 0, 1, tiled=True)]
    all_to_all x4 -> x0, starting transfers between devices: 29.7 us -> none  [the longest x1 11.3 us: local_op(): diag_new = lax.all_to_all(diag_mid, 'col', 0, 1, tiled=True)]
    convert_element_type x4 -> x0, local copies, waits for them, and re-layouts: 29.6 us -> none  [the longest x1 9.39 us: local_op(): mode_product(a_three, volume, 'ka,ijar->ijkr').astype(jnp.bfloat16)]
    dot_general x5 -> x0, matrix products: 20.6 us -> none  [mode_product(): return jnp.einsum(form, factor, tensor, preferred_element_type=jnp.float32)]
  transfers between devices with their start and end apart: 4 -> 0, of which waited for: 1 -> 0; matrix products, arithmetic and copies ran while one was open for 22% -> 0% of each run, Pallas kernels for 0% -> 0%
where the time goes in v1:
time: 82.7 us; the launch traced here: 82.1 us
  Pallas kernels  74.5 us (90%)
  local copies, waits for them, and re-layouts  7.56 us (9%)
    pallas_call x1, Pallas kernels, exchange(): pl.pallas_call(exchange_kernel, out_shape=jax.ShapeDtypeStruct((2, HALF,...  67.7 us
    unnamed x16, local copies, waits for them, and re-layouts  7.56 us
    pallas_call x1, Pallas kernels, last(): pl.pallas_call(last_kernel, grid=(HALF // step,), out_shape=jax.ShapeDtyp...  6.76 us

profile of v1, /device:TPU:1, one launch (start us, length us, event | category | flops | bytes accessed | tf_op | source)
XLA Modules:
  0.0 82.1 jit_solution(1923731017859812576)
XLA Ops:
  0.0 0.0 copy-start.1
  0.0 1.6 %copy-done.1 = bf16[64,2,128,64]{2,3,1,0:T(8,128)(2,1)S(1)} copy-done((bf16[64,2,128,64]{2,3,1,0:T(8,128)(2,1)S(1)}, bf16[64,2,128,64]{2,3,1,0:T(8,128)(2,1)}, u32[]{:S(2)}) %copy-start.1) | copy-done | bytes 2097176
  1.6 0.0 copy-start.2
  1.6 0.8 %copy-done.2 = f32[64,2,128]{2,1,0:T(2,128)S(1)} copy-done((f32[64,2,128]{2,1,0:T(2,128)S(1)}, f32[64,2,128]{2,1,0:T(2,128)}, u32[]{:S(2)}) %copy-start.2) | copy-done | bytes 65560
  2.4 0.0 copy-start.3
  2.4 0.8 copy-done.3
  3.2 0.0 copy-start.4
  3.2 0.8 copy-done.4
  3.9 0.0 copy-start.5
  4.0 0.8 copy-done.5
  4.7 0.0 copy-start.6
  4.7 0.8 copy-done.6
  5.5 0.0 copy-start.7
  5.5 0.8 copy-done.7
  6.2 67.7 %exchange.1.v_ref = bf16[2,64,64,128]{3,2,1,0:T(8,128)(2,1)S(1)} custom-call(bf16[64,2,64,128]{3,2,1,0:T(8,128)(2,1)S(1)} %bitcast.2, bf16[128,128]{1,0:T(8,128)(2,1)S(1)} %copy-done.3, bf16[128,128]{1,0:T(8,128)(2,1)S(1)} %copy-done.4, bf16[128,128]{1,0:T(8,128)(2,1)S(1)} %copy-done.5, bf16[128,128]{1,0:T(8,128)(2,1)S(1)} %copy-done.6, ...), custom_call_target="tpu_custom_call" | custom-call | tf_op jit(solution)/shard_map/exchange/pallas_call | solution.py:214
  74.0 0.0 copy-start
  74.0 1.3 %copy-done = bf16[2,64,64,128]{3,2,1,0:T(8,128)(2,1)} copy-done((bf16[2,64,64,128]{3,2,1,0:T(8,128)(2,1)}, bf16[2,64,64,128]{3,2,1,0:T(8,128)(2,1)S(1)}, u32[]{:S(2)}) %copy-start) | copy-done | bytes 2097176
  75.3 6.8 %last.1 = f32[64,2,64,128]{3,2,1,0:T(8,128)} custom-call(bf16[2,64,64,128]{3,2,1,0:T(8,128)(2,1)} %copy-done, bf16[128,128]{1,0:T(8,128)(2,1)} %b3_ref.1), custom_call_target="tpu_custom_call" | custom-call | tf_op jit(solution)/shard_map/last/pallas_call | solution.py:248
Async XLA Ops:
  0.0 1.6 %copy-start.1 = (bf16[64,2,128,64]{2,3,1,0:T(8,128)(2,1)S(1)}, bf16[64,2,128,64]{2,3,1,0:T(8,128)(2,1)}, u32[]{:S(2)}) copy-start(bf16[64,2,128,64]{2,3,1,0:T(8,128)(2,1)} %param.8) | copy-start | bytes 6291460
  1.6 0.8 %copy-start.2 = (f32[64,2,128]{2,1,0:T(2,128)S(1)}, f32[64,2,128]{2,1,0:T(2,128)}, u32[]{:S(2)}) copy-start(f32[64,2,128]{2,1,0:T(2,128)} %d_ref.1) | copy-start | bytes 196612
  2.4 0.8 copy-start.3
  3.2 0.8 copy-start.4
  3.9 0.8 copy-start.5
  4.7 0.8 copy-start.6
  5.5 0.8 copy-start.7
  74.0 1.3 %copy-start = (bf16[2,64,64,128]{3,2,1,0:T(8,128)(2,1)}, bf16[2,64,64,128]{3,2,1,0:T(8,128)(2,1)S(1)}, u32[]{:S(2)}) copy-start(bf16[2,64,64,128]{3,2,1,0:T(8,128)(2,1)S(1)} %exchange.1.v_ref) | copy-start | bytes 6291460

commit v2 on v1

v2 whole, which is shorter than its diff:
```python
import functools

import jax
import jax.numpy as jnp
from jax import lax
from jax.experimental import pallas as pl
from jax.experimental.pallas import tpu as pltpu
from jax.sharding import PartitionSpec as P

MESH, LOGICAL = pl.DeviceIdType.MESH, pl.DeviceIdType.LOGICAL
BF = jnp.bfloat16
F32 = jnp.float32
N = 128
C = 64
NCH = 4
R = C // NCH
HALF = N // 2


def each_partner(me, act):
    def body(t, carry):
        base = lax.bitwise_xor(me, t * 8)
        for u in range(8):
            peer = lax.bitwise_xor(base, ((5 * u) % 16) * 8 + u)
            if u == 0:
                pl.when(t > 0)(functools.partial(act, peer))
            else:
                act(peer)
        return carry

    lax.fori_loop(0, 16, body, 0)


def by_rows(factor, stack):
    for r in range(0, stack.shape[0], 2):
        pair = jnp.concatenate([stack[r], stack[r + 1]], axis=1)
        yield jnp.dot(factor, pair, preferred_element_type=F32)


def restack(products):
    parts = []
    for p in products:
        parts += [p[:, :N], p[:, N:]]
    return jnp.swapaxes(jnp.stack(parts, axis=0), 0, 1)


def exchange_kernel(x_ref, a1_hbm, b1_hbm, a2_hbm, b2_hbm, a3_hbm, d_hbm, v_ref,
                    xv, us, uu, m1, r1, m2, r2, vs, dv,
                    a1_ref, b1_ref, a2_ref, b2_ref, a3_ref, d_ref,
                    xsem, fsem, us_s, us_r, d_s, d_r, s1, q1, s2, q2, v_s, v_r):
    col, row = lax.axis_index("col"), lax.axis_index("row")
    me = col * 2 + row
    other = 1 - row
    mine = row == col // (HALF // 2)

    loads = [pltpu.make_async_copy(a3_hbm, a3_ref, fsem.at[0])]
    for k in range(2):
        j = other if k == 0 else row
        loads.append(pltpu.make_async_copy(x_ref.at[:, pl.ds(j, 1)], xv.at[:, pl.ds(k, 1)], xsem.at[k]))
    loads += [
        pltpu.make_async_copy(a1_hbm, a1_ref, fsem.at[1]),
        pltpu.make_async_copy(d_hbm, d_ref, fsem.at[2]),
        pltpu.make_async_copy(a2_hbm, a2_ref, fsem.at[3]),
        pltpu.make_async_copy(b2_hbm, b2_ref, fsem.at[4]),
        pltpu.make_async_copy(b1_hbm.at[pl.ds(row * HALF, HALF)], b1_ref.at[pl.ds(0, HALF)], fsem.at[5]),
        pltpu.make_async_copy(b1_hbm.at[pl.ds(other * HALF, HALF)], b1_ref.at[pl.ds(HALF, HALF)], fsem.at[6]),
    ]
    for load in loads:
        load.start()

    barrier = pltpu.get_barrier_semaphore()

    def greet(peer):
        pl.semaphore_signal(barrier, inc=1, device_id=peer, device_id_type=LOGICAL)

    each_partner(me, greet)

    def mode_three(k, block, out):
        rows = xv[pl.ds(block * 16, 16), k].reshape(16 * C, N)
        u = lax.dot_general(rows, a3_ref[...], (((1,), (1,)), ((), ())), preferred_element_type=F32)
        out[pl.ds(block * 16 + (0 if k == 0 else row * HALF), 16)] = u.astype(BF).reshape(16, C, N)

    loads[0].wait()
    loads[1].wait()

    def three_a(b, carry):
        mode_three(0, b, us)
        return carry

    lax.fori_loop(0, 4, three_a, 0)
    loads[2].wait()

    def three_b(b, carry):
        mode_three(1, b, uu)
        return carry

    lax.fori_loop(0, 4, three_b, 0)
    for load in loads[3:]:
        load.wait()

    pl.semaphore_wait(barrier, N - 1)

    def swap_u(ch):
        part = pl.ds(pl.multiple_of(ch * R, R), R)
        return pltpu.make_async_remote_copy(
            src_ref=us.at[:, part], dst_ref=uu.at[pl.ds(row * HALF, HALF), part],
            send_sem=us_s.at[ch], recv_sem=us_r.at[ch],
            device_id=(0, col, other), device_id_type=MESH)

    for ch in range(NCH):
        swap_u(ch).start()

    low = lax.rem(me, HALF)

    def give_d(i):
        pltpu.make_async_remote_copy(
            src_ref=d_ref.at[i], dst_ref=dv.at[col], send_sem=d_s, recv_sem=d_r,
            device_id=row * HALF + i, device_id_type=LOGICAL).start()

    def send_d(t, carry):
        base = lax.bitwise_xor(low, t * 8)
        for u in range(8):
            i = lax.bitwise_xor(base, u)
            if u == 0:
                pl.when(jnp.logical_or(t > 0, jnp.logical_not(mine)))(functools.partial(give_d, i))
            else:
                give_d(i)
        return carry

    @pl.when(mine)
    def _():
        dv[col] = d_ref[low]

    lax.fori_loop(0, 8, send_d, 0)

    def fan_out(ch, src, dst, ssem, rsem):
        def send(peer):
            pltpu.make_async_remote_copy(
                src_ref=src.at[ch, peer], dst_ref=dst.at[ch, me],
                send_sem=ssem.at[ch], recv_sem=rsem.at[ch],
                device_id=peer, device_id_type=LOGICAL).start()

        each_partner(me, send)
        dst[ch, me] = src[ch, me]

    def wait_all(buf, ch, sem):
        whole = buf.at[ch, pl.ds(0, N - 1)]
        pltpu.make_async_copy(whole, whole, sem.at[ch]).wait()

    def first(ch, carry):
        swap_u(ch).wait_recv()
        part = pl.ds(pl.multiple_of(ch * R, R), R)
        stack = jnp.swapaxes(uu[:, part], 0, 1)
        m1[ch] = restack(p.astype(BF) for p in by_rows(a1_ref[...], stack))
        fan_out(ch, m1, r1, s1, q1)
        return carry

    lax.fori_loop(0, NCH, first, 0)

    @pl.when(mine)
    def _():
        part = dv.at[pl.ds(0, HALF - 1)]
        pltpu.make_async_copy(part, part, d_r).wait()

    @pl.when(jnp.logical_not(mine))
    def _():
        pltpu.make_async_copy(dv, dv, d_r).wait()

    def second(ch, carry):
        wait_all(r1, ch, q1)
        diag = dv[...].reshape(N, N)
        diag = jnp.concatenate([diag, diag], axis=1)
        stack = jnp.swapaxes(r1[ch], 0, 1)
        outs = []
        for p in by_rows(a2_ref[...], stack):
            w = (diag * p.astype(BF).astype(F32)).astype(BF)
            outs.append(jnp.dot(b2_ref[...], w, preferred_element_type=F32).astype(BF))
        m2[ch] = restack(outs)
        fan_out(ch, m2, r2, s2, q2)
        return carry

    lax.fori_loop(0, NCH, second, 0)

    def swap_v(ch):
        part = pl.ds(pl.multiple_of(ch * R, R), R)
        return pltpu.make_async_remote_copy(
            src_ref=vs.at[:, part], dst_ref=v_ref.at[row, :, part],
            send_sem=v_s.at[ch], recv_sem=v_r.at[ch],
            device_id=(0, col, other), device_id_type=MESH)

    def third(ch, carry):
        wait_all(r2, ch, q2)
        part = pl.ds(pl.multiple_of(ch * R, R), R)
        stack = jnp.swapaxes(r2[ch], 0, 1)
        v = restack(p.astype(BF) for p in by_rows(b1_ref[...], stack))
        vs[:, part] = v[HALF:]
        swap_v(ch).start()
        v_ref[row, :, part] = v[:HALF]
        return carry

    lax.fori_loop(0, NCH, third, 0)

    @pl.when(mine)
    def _():
        part = dv.at[pl.ds(0, HALF - 1)]
        pltpu.make_async_copy(part, part, d_s).wait()

    @pl.when(jnp.logical_not(mine))
    def _():
        pltpu.make_async_copy(dv, dv, d_s).wait()

    def drain(ch, carry):
        swap_u(ch).wait_send()
        wait_all(m1, ch, s1)
        wait_all(m2, ch, s2)
        swap_v(ch).wait()
        return carry

    lax.fori_loop(0, NCH, drain, 0)


def exchange(x, a1, b1, a2, b2, a3, d):
    dma = pltpu.SemaphoreType.DMA
    hbm = pl.BlockSpec(memory_space=pltpu.HBM)
    return pl.pallas_call(
        exchange_kernel,
        out_shape=jax.ShapeDtypeStruct((2, HALF, C, N), BF),
        in_specs=[hbm] * 7,
        out_specs=pl.BlockSpec(memory_space=pltpu.VMEM),
        scratch_shapes=[
            pltpu.VMEM((HALF, 2, C, N), BF),
            pltpu.VMEM((HALF, C, N), BF),
            pltpu.VMEM((N, C, N), BF),
            pltpu.VMEM((NCH, N, R, N), BF),
            pltpu.VMEM((NCH, N, R, N), BF),
            pltpu.VMEM((NCH, N, R, N), BF),
            pltpu.VMEM((NCH, N, R, N), BF),
            pltpu.VMEM((HALF, C, N), BF),
            pltpu.VMEM((HALF, 2, N), F32),
            *[pltpu.VMEM((N, N), BF)] * 5,
            pltpu.VMEM((HALF, 2, N), F32),
            dma((2,)), dma((7,)), dma((NCH,)), dma((NCH,)), dma, dma,
            dma((NCH,)), dma((NCH,)), dma((NCH,)), dma((NCH,)),
            dma((NCH,)), dma((NCH,)),
        ],
        compiler_params=pltpu.CompilerParams(
            collective_id=0, has_side_effects=True, vmem_limit_bytes=40 << 20),
        name="exchange",
    )(*[pltpu.with_memory_space_constraint(v, pltpu.HBM) for v in (x, a1, b1, a2, b2, a3, d)])


def last_kernel(v_ref, b3_ref, z_ref, zv, zsem):
    step = 8

    def out(b):
        part = pl.ds(b * step, step)
        return pltpu.make_async_copy(zv.at[part], z_ref.at[part], zsem)

    def body(b, carry):
        for j in range(2):
            rows = v_ref[j, pl.ds(b * step, step)].reshape(step * C, N)
            z = lax.dot_general(rows, b3_ref[...], (((1,), (1,)), ((), ())), preferred_element_type=F32)
            zv[pl.ds(b * step, step), j] = z.reshape(step, C, N)
        out(b).start()
        return carry

    lax.fori_loop(0, HALF // step, body, 0)
    pltpu.make_async_copy(zv, z_ref, zsem).wait()


def last(v, b3):
    vmem = pl.BlockSpec(memory_space=pltpu.VMEM)
    return pl.pallas_call(
        last_kernel,
        out_shape=jax.ShapeDtypeStruct((HALF, 2, C, N), F32),
        in_specs=[vmem, vmem],
        out_specs=pl.BlockSpec(memory_space=pltpu.HBM),
        scratch_shapes=[pltpu.VMEM((HALF, 2, C, N), F32), pltpu.SemaphoreType.DMA],
        compiler_params=pltpu.CompilerParams(vmem_limit_bytes=16 << 20),
        name="last",
    )(v, b3)


def solution(mesh):
    vol_spec = P("row", "col", None, "rhs")
    diag_spec = P("row", "col", None)
    full = P(None, None)

    def local_op(volume, a_one, b_one, a_two, b_two, a_three, b_three, spectrum):
        x = jnp.swapaxes(volume, 2, 3)
        v = exchange(x, a_one, b_one, a_two, b_two, a_three, spectrum)
        return jnp.swapaxes(last(v, b_three), 2, 3)

    return jax.shard_map(local_op, mesh=mesh, in_specs=(vol_spec,) + (full,) * 6 + (diag_spec,),
                         out_specs=vol_spec, check_vma=False)
```

time: 82.7 us -> 66.2 us (0.80)
  Pallas kernels: 74.5 us -> 66 us
  local copies, waits for them, and re-layouts: 7.56 us -> 0.01 us
    unnamed x16 -> x2, local copies, waits for them, and re-layouts: 7.56 us -> 0.01 us
    pallas_call x1, Pallas kernels: 67.7 us -> 63.4 us  [exchange(): pl.pallas_call(exchange_kernel, out_shape=jax.ShapeDtypeStruct((2, HALF,...]
    pallas_call x1, Pallas kernels: 6.76 us -> 2.62 us  [last(): pl.pallas_call(last_kernel, out_shape=jax.ShapeDtypeStruct((HALF, 2, C, N...]
where the time goes in v2:
time: 66.2 us; the launch traced here: 66.1 us
  Pallas kernels  66 us (100%)
    pallas_call x1, Pallas kernels, exchange(): pl.pallas_call(exchange_kernel, out_shape=jax.ShapeDtypeStruct((2, HALF,...  63.4 us
    pallas_call x1, Pallas kernels, last(): pl.pallas_call(last_kernel, out_shape=jax.ShapeDtypeStruct((HALF, 2, C, N...  2.62 us

profile of v2, /device:TPU:1, one launch (start us, length us, event | category | flops | bytes accessed | tf_op | source)
XLA Modules:
  0.0 66.1 jit_solution(2313185450821101961)
XLA Ops:
  0.0 0.0 copy-start
  0.0 63.4 %exchange.1.v_ref = bf16[2,64,64,128]{3,2,1,0:T(8,128)(2,1)S(1)} custom-call(bf16[64,2,64,128]{3,2,1,0:T(8,128)(2,1)} %bitcast.2, bf16[128,128]{1,0:T(8,128)(2,1)} %a1_hbm.1, bf16[128,128]{1,0:T(8,128)(2,1)} %b1_hbm.1, bf16[128,128]{1,0:T(8,128)(2,1)} %a2_hbm.1, bf16[128,128]{1,0:T(8,128)(2,1)} %b2_hbm.1, bf16[128,128]{1,0:T(8,128)(2,1)} %a3_hbm.1, ...), custom_call_target="tpu_custom_call" | custom-call | tf_op jit(solution)/shard_map/exchange/pallas_call | solution.py:225
  63.4 0.0 copy-done
  63.4 2.6 %last.1 = f32[64,2,64,128]{3,2,1,0:T(8,128)} custom-call(bf16[2,64,64,128]{3,2,1,0:T(8,128)(2,1)S(1)} %exchange.1.v_ref, bf16[128,128]{1,0:T(8,128)(2,1)S(1)} %copy-done), custom_call_target="tpu_custom_call" | custom-call | tf_op jit(solution)/shard_map/last/pallas_call | solution.py:273
Async XLA Ops:
  0.0 63.4 %copy-start = (bf16[128,128]{1,0:T(8,128)(2,1)S(1)}, bf16[128,128]{1,0:T(8,128)(2,1)}, u32[]{:S(2)}) copy-start(bf16[128,128]{1,0:T(8,128)(2,1)} %b3_ref.1) | copy-start | bytes 98308
